TPU v7x, 32 devices: a whole 2x2x4 slice. The times are simulated.
32 devices in a mesh: gx: 4 (over z), gy: 4 (over y, core), gz: 2 (over x).
Axes of the slice: x: 2, y: 2, z: 4, core: 2. Of those that a mesh axis runs over, the one named last changes fastest.
Arguments:
- coarse_source: float32 [64, 128, 256], P('gx', 'gy', 'gz'), may hold values from -6 to 6
- coarse_shift: float32 [64, 128, 256], P('gx', 'gy', 'gz'), may hold values from 0.1 to 4
- coarse_start: float32 [64, 128, 256], P('gx', 'gy', 'gz'), may hold values from -3 to 3
- fine_source: float32 [128, 32768], P(('gx', 'gy', 'gz')), may hold values from -6 to 6
- fine_shift: float32 [128, 32768], P(('gx', 'gy', 'gz')), may hold values from 0.1 to 4
- fine_start: float32 [128, 32768], P(('gx', 'gy', 'gz')), may hold values from -3 to 3
- box_corner: int32 [32, 4, 3], P(('gx', 'gy', 'gz')), may hold values from 0 to 480, as said below
- box_owner: int32 [32, 4], P(('gx', 'gy', 'gz')), may hold values from 0 to 8, as said below
Outputs:
- potential: float32 [64, 128, 256], P('gx', 'gy', 'gz')
- fine_solution: float32 [128, 32768], P(('gx', 'gy', 'gz'))
- residual_norms: float32 [2], replicated
Inputs may be any that keep to these rules, and one draw needn't show every extreme that they name: `box_owner`: each device has at least one live slot; in every group of 8 devices that share a gx index some device has 4 live slots; the live owners of one device are distinct; no device is the owner of more than 4 live boxes, and in every group some device is the owner of exactly 4 live boxes. `box_corner`: each corner is a multiple of 32 and its footprint lies in the coarse block of the device that lists it; the 4 footprints of one device are distinct.
All inputs are finite; a program needn't handle non-finite values.
Results may differ from a plain program's by a relative error of at most 0.0001.
Values sent between devices are 32-bit elements; how exact they have to be, the bound alone decides.
A program may use at most 128 MiB of HBM per device.

v0:
```python
import jax
import jax.numpy as jnp
from jax import lax
from jax.sharding import PartitionSpec as P

FOOT = 16
CYCLES = 2
CSWEEPS = 4
FSWEEPS = 3


OMEGA = 0.8
HIGHEST = lax.Precision.HIGHEST


def extended(block, sides, width):
    for axis, dim in sides:
        count = lax.axis_size(axis)
        forward = [(i, i + 1) for i in range(count - 1)]
        backward = [(target, source) for source, target in forward]
        low = lax.ppermute(
            lax.slice_in_dim(block, block.shape[dim] - width, None, axis=dim), axis, forward
        )
        high = lax.ppermute(lax.slice_in_dim(block, 0, width, axis=dim), axis, backward)
        block = jnp.concatenate([low, block, high], axis=dim)
    return block


def to_blocks(field):
    extent = field.shape
    shaped = field.reshape(
        extent[0] // FOOT, FOOT, extent[1] // FOOT, FOOT, extent[2] // FOOT, FOOT
    )
    return shaped.transpose(0, 2, 4, 1, 3, 5).reshape(-1, FOOT * FOOT * FOOT)


def from_blocks(blocks, extent):
    shaped = blocks.reshape(
        extent[0] // FOOT, extent[1] // FOOT, extent[2] // FOOT, FOOT, FOOT, FOOT
    )
    return shaped.transpose(0, 3, 1, 4, 2, 5).reshape(extent)


def inject(parents):
    number = parents.shape[0]
    shaped = parents.reshape(number, FOOT, 1, FOOT, 1, FOOT, 1)
    spread = jnp.broadcast_to(shaped, (number, FOOT, 2, FOOT, 2, FOOT, 2))
    return spread.reshape(number, 8 * FOOT * FOOT * FOOT)


def restrict(values):
    number = values.shape[0]
    return (
        values.reshape(number, FOOT, 2, FOOT, 2, FOOT, 2)
        .mean(axis=(2, 4, 6))
        .reshape(number, FOOT * FOOT * FOOT)
    )


def fine_residual(values, parents, source, shift):
    ghost = inject(parents)
    side = 2 * FOOT
    position = jnp.arange(side * side * side, dtype=jnp.int32)[None, :]
    summed = jnp.zeros_like(values)
    for stride in (1, side, side * side):
        coordinate = position // stride % side
        upper = jnp.roll(values, -stride, axis=1)
        lower = jnp.roll(values, stride, axis=1)
        summed = (
            summed
            + jnp.where(coordinate < side - 1, upper, ghost)
            + jnp.where(coordinate > 0, lower, ghost)
        )
    return source - (6.0 + shift) * values + summed


def beside_sum(padded):
    summed = padded[2:, 1:-1, 1:-1] + padded[:-2, 1:-1, 1:-1]
    summed = summed + padded[1:-1, 2:, 1:-1] + padded[1:-1, :-2, 1:-1]
    return summed + padded[1:-1, 1:-1, 2:] + padded[1:-1, 1:-1, :-2]


def edge_mask(start, count, total):
    coords = start - 2 + jnp.arange(count + 4, dtype=jnp.int32)
    return (coords >= 0) & (coords < total)


def inside_mask(extent):
    mask_x = edge_mask(lax.axis_index("gx") * extent[0], extent[0], extent[0] * lax.axis_size("gx"))
    mask_y = edge_mask(lax.axis_index("gy") * extent[1], extent[1], extent[1] * lax.axis_size("gy"))
    mask_z = edge_mask(lax.axis_index("gz") * extent[2], extent[2], extent[2] * lax.axis_size("gz"))
    return mask_x[:, None, None] & mask_y[None, :, None] & mask_z[None, None, :]


def local(
    coarse_source,
    coarse_shift,
    coarse_start,
    fine_source,
    fine_shift,
    fine_start,
    box_corner,
    box_owner,
):
    extent = coarse_source.shape
    size_y = lax.axis_size("gy")
    size_z = lax.axis_size("gz")
    group = size_y * size_z
    slots = box_owner.shape[1]
    anchor = jnp.stack(
        [
            lax.axis_index("gx") * extent[0],
            lax.axis_index("gy") * extent[1],
            lax.axis_index("gz") * extent[2],
        ]
    )
    along_y = extent[1] // FOOT
    along_z = extent[2] // FOOT
    places = extent[0] // FOOT * along_y * along_z
    block = (box_corner[0] // 2 - anchor[None, :]) // FOOT
    location = (block[:, 0] * along_y + block[:, 1]) * along_z + block[:, 2]
    live = (box_owner[0] < group).astype(jnp.float32)
    peer_ids = jnp.arange(group, dtype=jnp.int32)
    route = (box_owner[0][None, :] == peer_ids[:, None]).astype(jnp.float32) * live[None, :]
    locate = (jnp.arange(places, dtype=jnp.int32)[:, None] == location[None, :]).astype(jnp.float32)
    collect = jnp.dot(route, locate.T, precision=HIGHEST)
    deposit = collect.T
    live_out = jnp.sum(route, axis=1, keepdims=True)
    diagonal = 6.0 + coarse_shift
    fine_diagonal = 6.0 + fine_shift

    def send_parents(potential):
        outgoing = jnp.dot(collect, to_blocks(potential), precision=HIGHEST)
        parents, flags = (
            lax.all_to_all(outgoing, ("gy", "gz"), split_axis=0, concat_axis=0, tiled=True),
            lax.all_to_all(live_out, ("gy", "gz"), split_axis=0, concat_axis=0, tiled=True),
        )
        return (parents, flags)

    inside = inside_mask(extent)
    inner = inside[1:-1, 1:-1, 1:-1]
    shift_wide = extended(diagonal, (("gx", 0), ("gy", 1), ("gz", 2)), 2)
    scale = jnp.where(inside, shift_wide, 6.0)
    scale_inner = scale[1:-1, 1:-1, 1:-1]
    potential = coarse_start
    values = fine_start
    earlier = None
    norms = []
    pick = None
    occupied = None
    for cycle in range(CYCLES):
        received, flags = send_parents(potential)
        if pick is None:
            flag_vec = flags[:, 0]
            before = jnp.cumsum(flag_vec) - flag_vec
            pick = (jnp.arange(slots, dtype=jnp.float32)[:, None] == before[None, :]).astype(
                jnp.float32
            ) * flag_vec[None, :]
            occupied = jnp.sum(pick, axis=1, keepdims=True)
        parents = jnp.dot(pick, received, precision=HIGHEST)
        if cycle > 0:
            values = values + inject(parents - earlier)
        for sweep in range(FSWEEPS):
            values = (
                values
                + OMEGA * fine_residual(values, parents, fine_source, fine_shift) / fine_diagonal
            )
        remainder = fine_residual(values, parents, fine_source, fine_shift)
        sent_back = jnp.dot(pick.T, restrict(remainder) * occupied, precision=HIGHEST)
        returned = lax.all_to_all(sent_back, ("gy", "gz"), split_axis=0, concat_axis=0, tiled=True)
        composite = coarse_source + from_blocks(
            jnp.dot(deposit, returned, precision=HIGHEST), extent
        )
        smooth_potential = potential
        source_wide = extended(composite, (("gx", 0), ("gy", 1), ("gz", 2)), 2)
        source_inner = source_wide[1:-1, 1:-1, 1:-1]
        for sweep_pair in range(CSWEEPS // 2):
            field = extended(smooth_potential, (("gx", 0), ("gy", 1), ("gz", 2)), 2)
            centre = field[1:-1, 1:-1, 1:-1]
            first = source_inner - scale_inner * centre + beside_sum(field)
            middle = jnp.where(inner, centre + OMEGA * first / scale_inner, 0.0)
            residual = composite - diagonal * middle[1:-1, 1:-1, 1:-1] + beside_sum(middle)
            smooth_potential = middle[1:-1, 1:-1, 1:-1] + OMEGA * residual / diagonal
        potential = smooth_potential
        squares = jnp.sum(residual * residual)
        local_sum = squares + jnp.sum(occupied * remainder * remainder)
        norms.append(lax.psum(local_sum, ("gx", "gy", "gz")))
        earlier = parents
    received, flags = send_parents(potential)
    parents = jnp.dot(pick, received, precision=HIGHEST)
    values = (values + inject(parents - earlier)) * occupied
    cells = float(extent[0] * extent[1] * extent[2] * lax.axis_size("gx") * size_y * size_z)
    return (potential, values, jnp.sqrt(jnp.stack(norms) / cells))


def solution(mesh):
    in_specs = (
        P("gx", "gy", "gz"),
        P("gx", "gy", "gz"),
        P("gx", "gy", "gz"),
        P(("gx", "gy", "gz"), None),
        P(("gx", "gy", "gz"), None),
        P(("gx", "gy", "gz"), None),
        P(("gx", "gy", "gz"), None, None),
        P(("gx", "gy", "gz"), None),
    )
    out_specs = (P("gx", "gy", "gz"), P(("gx", "gy", "gz"), None), P())
    return jax.shard_map(local, mesh=mesh, in_specs=in_specs, out_specs=out_specs, check_vma=False)
```

profile of v0, /device:TPU:0, one launch (start us, length us, event | category | flops | bytes accessed | tf_op | source)
XLA Modules:
  0.0 499.2 jit_solution(5402457770921700320)
XLA Ops:
  2.1 4.9 collective-permute-start
  17.0 5.2 %collective-permute-start.12 = (f32[2,32,128]{2,1,0:T(8,128)}, f32[2,32,128]{2,1,0:T(8,128)S(1)}, u32[]{:S(2)}, u32[]{:S(2)}) collective-permute-start(f32[2,32,128]{2,1,0:T(8,128)} %get-tuple-element.158), channel_id=1, source_target_pairs={{0,8},{8,16},{16,24},{1,9},{9,17},{17,25},{2,10},{10,18},{18,26},{... | collective-permute-start | bytes 98312 | tf_op jit(solution)/shard_map/ppermute | solution.py:21
  49.6 4.9 collective-permute-start.14
  56.3 9.7 %broadcast_in_dim.322 = f32[4,16,2,16,2,16,2]{0,6,5,4,3,2,1:T(2,128)} broadcast(f32[4,16,16,16]{0,3,2,1:T(8,128)S(1)} %bitcast.135), dimensions={0,1,3,5} | broadcast | bytes 589824 | tf_op jit(solution)/shard_map/broadcast_in_dim | solution.py:47
  66.1 9.6 %copy.581 = f32[4,32768]{1,0:T(4,128)S(1)} copy(f32[4,32768]{0,1:T(8,128)} %bitcast.128) | data formatting | bytes 1048576 | tf_op jit(solution)/shard_map/reshape | solution.py:48
  90.3 8.6 %copy.605 = f32[4,32768]{0,1:T(8,128)} copy(f32[4,32768]{1,0:T(4,128)S(1)} %fusion.70) | data formatting | bytes 1048576 | tf_op jit(solution)/shard_map/add | solution.py:74
  98.9 13.6 %reduce_sum.77 = f32[4,16,16,16]{0,3,2,1:T(8,128)} reduce(f32[4,16,2,16,2,16,2]{0,6,5,4,3,2,1:T(2,128)} %bitcast.132, f32[]{:T(128)} %constant.236.clone.1), dimensions={2,4,6}, to_apply=%region_2.3 | reduce | flops 114688 | bytes 589828 | tf_op jit(solution)/shard_map/reduce_sum | solution.py:55
  122.0 4.4 collective-permute-start.4
  137.6 4.5 collective-permute-start.6
  149.8 5.5 %collective-permute-start.16 = (f32[20,36,2]{2,1,0:T(8,128)S(1)}, f32[20,36,2]{2,1,0:T(8,128)S(1)}, u32[]{:S(2)}, u32[]{:S(2)}) collective-permute-start(f32[20,36,2]{2,1,0:T(8,128)S(1)} %get-tuple-element.130), channel_id=1, source_target_pairs={{0,1},{2,3},{4,5},{6,7},{8,9},{10,11},{12,13},{14,15},{16,17},{18,... | collective-permute-start | bytes 17288 | tf_op jit(solution)/shard_map/ppermute | solution.py:21
  156.8 4.6 collective-permute-start.10
  164.9 6.9 %collective-permute-done.11 = f32[20,36,2]{2,1,0:T(8,128)S(1)} collective-permute-done((f32[20,36,2]{2,1,0:T(8,128)S(1)}, f32[20,36,2]{2,1,0:T(8,128)S(1)}, u32[]{:S(2)}, u32[]{:S(2)}) %collective-permute-start.11) | collective-permute-done | bytes 5792 | tf_op jit(solution)/shard_map/ppermute | solution.py:24
  173.7 5.1 %fusion.37 = (f32[18,34,130]{2,1,0:T(8,128)S(1)}, f32[18,34,130]{2,1,0:T(8,128)S(1)}) fusion(f32[20,36,2]{2,1,0:T(8,128)} %collective-permute-done.4, f32[20,2,128]{2,1,0:T(2,128)S(1)} %copy-done.25, f32[20,32,128]{2,1,0:T(8,128)S(1)} %copy-done.10, f32[20,2,128]{2,1,0:T(2,128)S(1)} %copy-done.27, f32[20,36,2]{2,1,0:T(8,128)} %collective-permute-done.5, ...), kind=kLoop, calls=%fused_computation.104 | loop fusion | flops 2466360 | bytes 3447720 | tf_op jit(solution)/shard_map/jit(_where)/select_n | solution.py:181
  180.7 4.9 collective-permute-start.18
  192.5 4.4 collective-permute-start.22
  198.7 7.6 %collective-permute-done.22 = f32[20,36,2]{2,1,0:T(8,128)S(1)} collective-permute-done((f32[20,36,2]{2,1,0:T(8,128)S(1)}, f32[20,36,2]{2,1,0:T(8,128)S(1)}, u32[]{:S(2)}, u32[]{:S(2)}) %collective-permute-start.22) | collective-permute-done | bytes 5792 | tf_op jit(solution)/shard_map/ppermute | solution.py:21
  229.0 5.4 %collective-permute-start.24 = (f32[2,32,128]{2,1,0:T(8,128)}, f32[2,32,128]{2,1,0:T(8,128)}, u32[]{:S(2)}, u32[]{:S(2)}) collective-permute-start(f32[2,32,128]{2,1,0:T(8,128)} %get-tuple-element.154), channel_id=1, source_target_pairs={{0,8},{8,16},{16,24},{1,9},{9,17},{17,25},{2,10},{10,18},{18,26},{... | collective-permute-start | bytes 98312 | tf_op jit(solution)/shard_map/ppermute | solution.py:21
  237.3 10.4 %broadcast_in_dim.331 = f32[4,16,2,16,2,16,2]{0,6,5,4,3,2,1:T(2,128)} broadcast(f32[4,16,16,16]{0,3,2,1:T(8,128)} %bitcast.133), dimensions={0,1,3,5} | broadcast | bytes 589824 | tf_op jit(solution)/shard_map/broadcast_in_dim | solution.py:47
  247.7 9.5 %copy.613 = f32[4,32768]{1,0:T(4,128)S(1)} copy(f32[4,32768]{0,1:T(8,128)} %bitcast.129) | data formatting | bytes 1048576 | tf_op jit(solution)/shard_map/reshape | solution.py:48
  264.7 10.4 %broadcast_in_dim.333 = f32[4,16,2,16,2,16,2]{0,6,5,4,3,2,1:T(2,128)} broadcast(f32[4,16,16,16]{0,3,2,1:T(8,128)} %bitcast.136), dimensions={0,1,3,5} | broadcast | bytes 589824 | tf_op jit(solution)/shard_map/broadcast_in_dim | solution.py:47
  275.0 9.5 %copy.615 = f32[4,32768]{1,0:T(4,128)S(1)} copy(f32[4,32768]{0,1:T(8,128)} %bitcast.130) | data formatting | bytes 1048576 | tf_op jit(solution)/shard_map/reshape | solution.py:48
  300.8 9.1 %copy.639 = f32[4,32768]{0,1:T(8,128)} copy(f32[4,32768]{1,0:T(4,128)} %get-tuple-element.21) | data formatting | bytes 1048576 | tf_op jit(solution)/shard_map/add | solution.py:74
  309.9 13.8 %reduce_sum.80 = f32[4,16,16,16]{0,3,2,1:T(8,128)} reduce(f32[4,16,2,16,2,16,2]{0,6,5,4,3,2,1:T(2,128)} %bitcast.127, f32[]{:T(128)} %constant.236.clone.1), dimensions={2,4,6}, to_apply=%region_4.5 | reduce | flops 114688 | bytes 589828 | tf_op jit(solution)/shard_map/reduce_sum | solution.py:55
  347.4 4.5 collective-permute-start.30
  365.1 4.6 collective-permute-start.34
  371.3 4.8 collective-permute-done.29
  377.4 7.5 %collective-permute-done.35 = f32[20,36,2]{2,1,0:T(8,128)S(1)} collective-permute-done((f32[20,36,2]{2,1,0:T(8,128)S(1)}, f32[20,36,2]{2,1,0:T(8,128)S(1)}, u32[]{:S(2)}, u32[]{:S(2)}) %collective-permute-start.35) | collective-permute-done | bytes 5792 | tf_op jit(solution)/shard_map/ppermute | solution.py:24
  389.5 5.2 %collective-permute-start.36 = (f32[2,32,128]{2,1,0:T(8,128)S(1)}, f32[2,32,128]{2,1,0:T(8,128)S(1)}, u32[]{:S(2)}, u32[]{:S(2)}) collective-permute-start(f32[2,32,128]{2,1,0:T(8,128)S(1)} %get-tuple-element.150), channel_id=1, source_target_pairs={{0,8},{8,16},{16,24},{1,9},{9,17},{17,25},{2,10},{10,18},{18,26},{... | collective-permute-start | bytes 98312 | tf_op jit(solution)/shard_map/ppermute | solution.py:21
  404.8 8.1 %collective-permute-done.40 = f32[20,36,2]{2,1,0:T(8,128)S(1)} collective-permute-done((f32[20,36,2]{2,1,0:T(8,128)S(1)}, f32[20,36,2]{2,1,0:T(8,128)S(1)}, u32[]{:S(2)}, u32[]{:S(2)}) %collective-permute-start.40) | collective-permute-done | bytes 5792 | tf_op jit(solution)/shard_map/ppermute | solution.py:21
  433.0 43.1 %all-reduce = (f32[1]{0:T(128)}, f32[1]{0:T(128)}) all-reduce(f32[1]{0:T(128)} %bitcast.40, f32[1]{0:T(128)} %bitcast.39), channel_id=1, replica_groups=mesh['gx'=4,'gy'=4,'gz'=2] {'gx','gy','gz'}, use_global_device_ids=true, to_apply=%region_10.11 | all-reduce | flops 2 | bytes 16 | tf_op jit(solution)/shard_map/psum | solution.py:187
  478.9 9.5 %broadcast_in_dim.335 = f32[4,16,2,16,2,16,2]{0,6,5,4,3,2,1:T(2,128)} broadcast(f32[4,16,16,16]{0,3,2,1:T(8,128)S(1)} %bitcast.134), dimensions={0,1,3,5} | broadcast | bytes 589824 | tf_op jit(solution)/shard_map/broadcast_in_dim | solution.py:47
  488.3 9.5 %copy.647 = f32[4,32768]{1,0:T(4,128)S(1)} copy(f32[4,32768]{0,1:T(8,128)} %bitcast.131) | data formatting | bytes 1048576 | tf_op jit(solution)/shard_map/reshape | solution.py:48
  (351 shorter events, 224.8 us)
Async XLA Ops:
  2.1 41.1 %collective-permute-start = (f32[2,32,128]{2,1,0:T(8,128)}, f32[2,32,128]{2,1,0:T(8,128)S(1)}, u32[]{:S(2)}, u32[]{:S(2)}) collective-permute-start(f32[2,32,128]{2,1,0:T(8,128)} %get-tuple-element.163), channel_id=1, source_target_pairs={{0,8},{8,16},{16,24},{1,9},{9,17},{17,25},{2,10},{10,18},{18,26},{... | collective-permute-start | bytes 98312 | tf_op jit(solution)/shard_map/ppermute | solution.py:21
  7.0 36.2 %collective-permute-start.1 = (f32[2,32,128]{2,1,0:T(8,128)}, f32[2,32,128]{2,1,0:T(8,128)S(1)}, u32[]{:S(2)}, u32[]{:S(2)}) collective-permute-start(f32[2,32,128]{2,1,0:T(8,128)} %get-tuple-element.162), channel_id=1, source_target_pairs={{8,0},{16,8},{24,16},{9,1},{17,9},{25,17},{10,2},{18,10},{26,18},{... | collective-permute-start | bytes 98312 | tf_op jit(solution)/shard_map/ppermute | solution.py:24
  10.4 26.3 %all-to-all-start = ((f32[8,1,1]{2,1,0:T(1,128)}), f32[8,1,1]{2,1,0:T(1,128)S(1)}, u32[]{:S(2)}, u32[]{:S(2)}) async-start(f32[8,1,1]{2,1,0:T(1,128)} %copy.577), calls=%async_computation | async-start | bytes 8192 | tf_op jit(solution)/shard_map/all_to_all | solution.py:136
  15.7 31.9 %collective-permute-start.13 = (f32[2,32,128]{2,1,0:T(8,128)}, f32[2,32,128]{2,1,0:T(8,128)S(1)}, u32[]{:S(2)}, u32[]{:S(2)}) collective-permute-start(f32[2,32,128]{2,1,0:T(8,128)} %get-tuple-element.159), channel_id=1, source_target_pairs={{8,0},{16,8},{24,16},{9,1},{17,9},{25,17},{10,2},{18,10},{26,18},{... | collective-permute-start | bytes 98312 | tf_op jit(solution)/shard_map/ppermute | solution.py:24
  17.0 30.7 %collective-permute-start.12 = (f32[2,32,128]{2,1,0:T(8,128)}, f32[2,32,128]{2,1,0:T(8,128)S(1)}, u32[]{:S(2)}, u32[]{:S(2)}) collective-permute-start(f32[2,32,128]{2,1,0:T(8,128)} %get-tuple-element.158), channel_id=1, source_target_pairs={{0,8},{8,16},{16,24},{1,9},{9,17},{17,25},{2,10},{10,18},{18,26},{... | collective-permute-start | bytes 98312 | tf_op jit(solution)/shard_map/ppermute | solution.py:21
  37.3 18.0 %all-to-all-start.1 = ((f32[8,1,4096]{2,1,0:T(1,128)}), f32[8,1,4096]{2,1,0:T(1,128)S(1)}, u32[]{:S(2)}, u32[]{:S(2)}) async-start(f32[8,1,4096]{2,1,0:T(1,128)} %copy.579), calls=%async_computation.1 | async-start | bytes 262144 | tf_op jit(solution)/shard_map/all_to_all | solution.py:135
  43.3 11.2 %collective-permute-start.3 = (f32[20,2,128]{2,1,0:T(2,128)S(1)}, f32[20,2,128]{2,1,0:T(2,128)S(1)}, u32[]{:S(2)}, u32[]{:S(2)}) collective-permute-start(f32[20,2,128]{2,1,0:T(2,128)S(1)} %get-tuple-element.149), channel_id=1, source_target_pairs={{2,0},{4,2},{6,4},{3,1},{5,3},{7,5},{10,8},{12,10},{14,12},{11,9},... | collective-permute-start | bytes 61448 | tf_op jit(solution)/shard_map/ppermute | solution.py:24
  48.3 89.2 %collective-permute-start.15 = (f32[20,2,128]{2,1,0:T(2,128)}, f32[20,2,128]{2,1,0:T(2,128)}, u32[]{:S(2)}, u32[]{:S(2)}) collective-permute-start(f32[20,2,128]{2,1,0:T(2,128)} %get-tuple-element.145), channel_id=1, source_target_pairs={{2,0},{4,2},{6,4},{3,1},{5,3},{7,5},{10,8},{12,10},{14,12},{11,9},... | collective-permute-start | bytes 61448 | tf_op jit(solution)/shard_map/ppermute | solution.py:24
  49.6 92.5 %collective-permute-start.14 = (f32[20,2,128]{2,1,0:T(2,128)}, f32[20,2,128]{2,1,0:T(2,128)}, u32[]{:S(2)}, u32[]{:S(2)}) collective-permute-start(f32[20,2,128]{2,1,0:T(2,128)} %get-tuple-element.144), channel_id=1, source_target_pairs={{0,2},{2,4},{4,6},{1,3},{3,5},{5,7},{8,10},{10,12},{12,14},{9,11},... | collective-permute-start | bytes 61448 | tf_op jit(solution)/shard_map/ppermute | solution.py:21
  117.0 10.7 %all-to-all-start.2 = ((f32[8,1,4096]{2,1,0:T(1,128)}), f32[8,1,4096]{2,1,0:T(1,128)S(1)}, u32[]{:S(2)}, u32[]{:S(2)}) async-start(f32[8,1,4096]{2,1,0:T(1,128)} %copy.606), calls=%async_computation.2 | async-start | bytes 262144 | tf_op jit(solution)/shard_map/all_to_all | solution.py:170
  122.0 34.8 %collective-permute-start.4 = (f32[20,36,2]{2,1,0:T(8,128)}, f32[20,36,2]{2,1,0:T(8,128)}, u32[]{:S(2)}, u32[]{:S(2)}) collective-permute-start(f32[20,36,2]{2,1,0:T(8,128)} %get-tuple-element.135), channel_id=1, source_target_pairs={{0,1},{2,3},{4,5},{6,7},{8,9},{10,11},{12,13},{14,15},{16,17},{18,... | collective-permute-start | bytes 17288 | tf_op jit(solution)/shard_map/ppermute | solution.py:21
  126.4 35.0 %collective-permute-start.5 = (f32[20,36,2]{2,1,0:T(8,128)}, f32[20,36,2]{2,1,0:T(8,128)}, u32[]{:S(2)}, u32[]{:S(2)}) collective-permute-start(f32[20,36,2]{2,1,0:T(8,128)} %get-tuple-element.134), channel_id=1, source_target_pairs={{1,0},{3,2},{5,4},{7,6},{9,8},{11,10},{13,12},{15,14},{17,16},{19,... | collective-permute-start | bytes 17288 | tf_op jit(solution)/shard_map/ppermute | solution.py:24
  145.2 10.0 %collective-permute-start.8 = (f32[20,2,128]{2,1,0:T(2,128)S(1)}, f32[20,2,128]{2,1,0:T(2,128)S(1)}, u32[]{:S(2)}, u32[]{:S(2)}) collective-permute-start(f32[20,2,128]{2,1,0:T(2,128)S(1)} %get-tuple-element.146), channel_id=1, source_target_pairs={{0,2},{2,4},{4,6},{1,3},{3,5},{5,7},{8,10},{10,12},{12,14},{9,11},... | collective-permute-start | bytes 61448 | tf_op jit(solution)/shard_map/ppermute | solution.py:21
  148.4 14.6 %collective-permute-start.17 = (f32[20,36,2]{2,1,0:T(8,128)S(1)}, f32[20,36,2]{2,1,0:T(8,128)S(1)}, u32[]{:S(2)}, u32[]{:S(2)}) collective-permute-start(f32[20,36,2]{2,1,0:T(8,128)S(1)} %get-tuple-element.131), channel_id=1, source_target_pairs={{1,0},{3,2},{5,4},{7,6},{9,8},{11,10},{13,12},{15,14},{17,16},{19,... | collective-permute-start | bytes 17288 | tf_op jit(solution)/shard_map/ppermute | solution.py:24
  149.8 15.2 %collective-permute-start.16 = (f32[20,36,2]{2,1,0:T(8,128)S(1)}, f32[20,36,2]{2,1,0:T(8,128)S(1)}, u32[]{:S(2)}, u32[]{:S(2)}) collective-permute-start(f32[20,36,2]{2,1,0:T(8,128)S(1)} %get-tuple-element.130), channel_id=1, source_target_pairs={{0,1},{2,3},{4,5},{6,7},{8,9},{10,11},{12,13},{14,15},{16,17},{18,... | collective-permute-start | bytes 17288 | tf_op jit(solution)/shard_map/ppermute | solution.py:21
  155.5 16.3 %collective-permute-start.11 = (f32[20,36,2]{2,1,0:T(8,128)S(1)}, f32[20,36,2]{2,1,0:T(8,128)S(1)}, u32[]{:S(2)}, u32[]{:S(2)}) collective-permute-start(f32[20,36,2]{2,1,0:T(8,128)S(1)} %get-tuple-element.133), channel_id=1, source_target_pairs={{1,0},{3,2},{5,4},{7,6},{9,8},{11,10},{13,12},{15,14},{17,16},{19,... | collective-permute-start | bytes 17288 | tf_op jit(solution)/shard_map/ppermute | solution.py:24
  156.8 16.9 %collective-permute-start.10 = (f32[20,36,2]{2,1,0:T(8,128)S(1)}, f32[20,36,2]{2,1,0:T(8,128)S(1)}, u32[]{:S(2)}, u32[]{:S(2)}) collective-permute-start(f32[20,36,2]{2,1,0:T(8,128)S(1)} %get-tuple-element.132), channel_id=1, source_target_pairs={{0,1},{2,3},{4,5},{6,7},{8,9},{10,11},{12,13},{14,15},{16,17},{18,... | collective-permute-start | bytes 17288 | tf_op jit(solution)/shard_map/ppermute | solution.py:21
  192.5 13.8 %collective-permute-start.22 = (f32[20,36,2]{2,1,0:T(8,128)S(1)}, f32[20,36,2]{2,1,0:T(8,128)S(1)}, u32[]{:S(2)}, u32[]{:S(2)}) collective-permute-start(f32[20,36,2]{2,1,0:T(8,128)S(1)} %get-tuple-element.129), channel_id=1, source_target_pairs={{0,1},{2,3},{4,5},{6,7},{8,9},{10,11},{12,13},{14,15},{16,17},{18,... | collective-permute-start | bytes 17288 | tf_op jit(solution)/shard_map/ppermute | solution.py:21
  197.0 13.5 %collective-permute-start.23 = (f32[20,36,2]{2,1,0:T(8,128)S(1)}, f32[20,36,2]{2,1,0:T(8,128)S(1)}, u32[]{:S(2)}, u32[]{:S(2)}) collective-permute-start(f32[20,36,2]{2,1,0:T(8,128)S(1)} %get-tuple-element.128), channel_id=1, source_target_pairs={{1,0},{3,2},{5,4},{7,6},{9,8},{11,10},{13,12},{15,14},{17,16},{19,... | collective-permute-start | bytes 17288 | tf_op jit(solution)/shard_map/ppermute | solution.py:24
  223.7 10.7 %all-to-all-start.3 = ((f32[8,1,4096]{2,1,0:T(1,128)}), f32[8,1,4096]{2,1,0:T(1,128)S(1)}, u32[]{:S(2)}, u32[]{:S(2)}) async-start(f32[8,1,4096]{2,1,0:T(1,128)} %copy.611), calls=%async_computation.3 | async-start | bytes 262144 | tf_op jit(solution)/shard_map/all_to_all | solution.py:135
  227.7 104.7 %collective-permute-start.25 = (f32[2,32,128]{2,1,0:T(8,128)}, f32[2,32,128]{2,1,0:T(8,128)}, u32[]{:S(2)}, u32[]{:S(2)}) collective-permute-start(f32[2,32,128]{2,1,0:T(8,128)} %get-tuple-element.155), channel_id=1, source_target_pairs={{8,0},{16,8},{24,16},{9,1},{17,9},{25,17},{10,2},{18,10},{26,18},{... | collective-permute-start | bytes 98312 | tf_op jit(solution)/shard_map/ppermute | solution.py:24
  229.0 103.4 %collective-permute-start.24 = (f32[2,32,128]{2,1,0:T(8,128)}, f32[2,32,128]{2,1,0:T(8,128)}, u32[]{:S(2)}, u32[]{:S(2)}) collective-permute-start(f32[2,32,128]{2,1,0:T(8,128)} %get-tuple-element.154), channel_id=1, source_target_pairs={{0,8},{8,16},{16,24},{1,9},{9,17},{17,25},{2,10},{10,18},{18,26},{... | collective-permute-start | bytes 98312 | tf_op jit(solution)/shard_map/ppermute | solution.py:21
  333.2 18.8 %collective-permute-start.27 = (f32[20,2,128]{2,1,0:T(2,128)S(1)}, f32[20,2,128]{2,1,0:T(2,128)S(1)}, u32[]{:S(2)}, u32[]{:S(2)}) collective-permute-start(f32[20,2,128]{2,1,0:T(2,128)S(1)} %get-tuple-element.141), channel_id=1, source_target_pairs={{2,0},{4,2},{6,4},{3,1},{5,3},{7,5},{10,8},{12,10},{14,12},{11,9},... | collective-permute-start | bytes 61448 | tf_op jit(solution)/shard_map/ppermute | solution.py:24
  334.5 17.5 %collective-permute-start.26 = (f32[20,2,128]{2,1,0:T(2,128)S(1)}, f32[20,2,128]{2,1,0:T(2,128)S(1)}, u32[]{:S(2)}, u32[]{:S(2)}) collective-permute-start(f32[20,2,128]{2,1,0:T(2,128)S(1)} %get-tuple-element.140), channel_id=1, source_target_pairs={{0,2},{2,4},{4,6},{1,3},{3,5},{5,7},{8,10},{10,12},{12,14},{9,11},... | collective-permute-start | bytes 61448 | tf_op jit(solution)/shard_map/ppermute | solution.py:21
  353.5 10.0 %collective-permute-start.33 = (f32[20,2,128]{2,1,0:T(2,128)S(1)}, f32[20,2,128]{2,1,0:T(2,128)S(1)}, u32[]{:S(2)}, u32[]{:S(2)}) collective-permute-start(f32[20,2,128]{2,1,0:T(2,128)S(1)} %get-tuple-element.139), channel_id=1, source_target_pairs={{2,0},{4,2},{6,4},{3,1},{5,3},{7,5},{10,8},{12,10},{14,12},{11,9},... | collective-permute-start | bytes 61448 | tf_op jit(solution)/shard_map/ppermute | solution.py:24
  358.1 13.2 %collective-permute-start.28 = (f32[20,36,2]{2,1,0:T(8,128)S(1)}, f32[20,36,2]{2,1,0:T(8,128)S(1)}, u32[]{:S(2)}, u32[]{:S(2)}) collective-permute-start(f32[20,36,2]{2,1,0:T(8,128)S(1)} %get-tuple-element.127), channel_id=1, source_target_pairs={{0,1},{2,3},{4,5},{6,7},{8,9},{10,11},{12,13},{14,15},{16,17},{18,... | collective-permute-start | bytes 17288 | tf_op jit(solution)/shard_map/ppermute | solution.py:21
  362.1 14.1 %collective-permute-start.29 = (f32[20,36,2]{2,1,0:T(8,128)S(1)}, f32[20,36,2]{2,1,0:T(8,128)S(1)}, u32[]{:S(2)}, u32[]{:S(2)}) collective-permute-start(f32[20,36,2]{2,1,0:T(8,128)S(1)} %get-tuple-element.126), channel_id=1, source_target_pairs={{1,0},{3,2},{5,4},{7,6},{9,8},{11,10},{13,12},{15,14},{17,16},{19,... | collective-permute-start | bytes 17288 | tf_op jit(solution)/shard_map/ppermute | solution.py:24
  363.8 21.2 %collective-permute-start.35 = (f32[20,36,2]{2,1,0:T(8,128)S(1)}, f32[20,36,2]{2,1,0:T(8,128)S(1)}, u32[]{:S(2)}, u32[]{:S(2)}) collective-permute-start(f32[20,36,2]{2,1,0:T(8,128)S(1)} %get-tuple-element.125), channel_id=1, source_target_pairs={{1,0},{3,2},{5,4},{7,6},{9,8},{11,10},{13,12},{15,14},{17,16},{19,... | collective-permute-start | bytes 17288 | tf_op jit(solution)/shard_map/ppermute | solution.py:24
  365.1 19.9 %collective-permute-start.34 = (f32[20,36,2]{2,1,0:T(8,128)S(1)}, f32[20,36,2]{2,1,0:T(8,128)S(1)}, u32[]{:S(2)}, u32[]{:S(2)}) collective-permute-start(f32[20,36,2]{2,1,0:T(8,128)S(1)} %get-tuple-element.124), channel_id=1, source_target_pairs={{0,1},{2,3},{4,5},{6,7},{8,9},{10,11},{12,13},{14,15},{16,17},{18,... | collective-permute-start | bytes 17288 | tf_op jit(solution)/shard_map/ppermute | solution.py:21
  401.7 11.1 %collective-permute-start.40 = (f32[20,36,2]{2,1,0:T(8,128)S(1)}, f32[20,36,2]{2,1,0:T(8,128)S(1)}, u32[]{:S(2)}, u32[]{:S(2)}) collective-permute-start(f32[20,36,2]{2,1,0:T(8,128)S(1)} %get-tuple-element.123), channel_id=1, source_target_pairs={{0,1},{2,3},{4,5},{6,7},{8,9},{10,11},{12,13},{14,15},{16,17},{18,... | collective-permute-start | bytes 17288 | tf_op jit(solution)/shard_map/ppermute | solution.py:21
  403.2 13.8 %collective-permute-start.41 = (f32[20,36,2]{2,1,0:T(8,128)S(1)}, f32[20,36,2]{2,1,0:T(8,128)S(1)}, u32[]{:S(2)}, u32[]{:S(2)}) collective-permute-start(f32[20,36,2]{2,1,0:T(8,128)S(1)} %get-tuple-element.122), channel_id=1, source_target_pairs={{1,0},{3,2},{5,4},{7,6},{9,8},{11,10},{13,12},{15,14},{17,16},{19,... | collective-permute-start | bytes 17288 | tf_op jit(solution)/shard_map/ppermute | solution.py:24
  427.2 50.7 %all-to-all-start.5 = ((f32[8,1,4096]{2,1,0:T(1,128)}), f32[8,1,4096]{2,1,0:T(1,128)S(1)}, u32[]{:S(2)}, u32[]{:S(2)}) async-start(f32[8,1,4096]{2,1,0:T(1,128)} %copy.645), calls=%async_computation.5 | async-start | bytes 262144 | tf_op jit(solution)/shard_map/all_to_all | solution.py:135
  (69 other events, 824.9 us)
where the time goes:
time: 507 us; the launch traced here: 499 us
  local copies, waits for them, and re-layouts  159 us (31%)
  starting transfers between devices  138 us (27%)
  other arithmetic  86.4 us (17%)
  waiting for transfers between devices  54.9 us (11%)
  blocking collectives  43.1 us (9%)
  matrix products  13.1 us (3%)
  between operations  5.18 us (1%)
    ppermute x21, starting transfers between devices, extended(): lax.ppermute(lax.slice_in_dim(block, block.shape[dim] - width, None, axis...  86.7 us
    broadcast_in_dim x8, local copies, waits for them, and re-layouts, inject(): spread = jnp.broadcast_to(shaped, (number, FOOT, 2, FOOT, 2, FOOT, 2))  45.1 us
    psum x1, blocking collectives, local(): norms.append(lax.psum(local_sum, ('gx', 'gy', 'gz')))  43.1 us
    reshape x4, local copies, waits for them, and re-layouts, inject(): return spread.reshape(number, 8 * FOOT * FOOT * FOOT)  38 us
    ppermute x21, starting transfers between devices, extended(): lax.ppermute(lax.slice_in_dim(block, 0, width, axis=dim), axis, backward)  28.1 us
    ppermute x21, waiting for transfers between devices, extended(): lax.ppermute(lax.slice_in_dim(block, 0, width, axis=dim), axis, backward)  27.5 us
    reduce_sum x2, other arithmetic, restrict(): return values.reshape(number, FOOT, 2, FOOT, 2, FOOT, 2).mean(axis=(2, 4,...  27.5 us
    ppermute x21, waiting for transfers between devices, extended(): lax.ppermute(lax.slice_in_dim(block, block.shape[dim] - width, None, axis...  27.3 us
  transfers between devices with their start and end apart: 48, of which 16 were waited for; matrix products, arithmetic and copies ran while one was open for 41% of the time, Pallas kernels for 0%

commit v1 on v0

v1 whole, which is shorter than its diff:
```python
import functools

import jax
import jax.numpy as jnp
from jax import lax
from jax.experimental import pallas as pl
from jax.experimental.pallas import tpu as pltpu
from jax.sharding import PartitionSpec as P

FOOT = 16
CYCLES = 2
CSWEEPS = 4
FSWEEPS = 3
OMEGA = 0.8
KEEP = 1.0 - OMEGA
MESH = pl.DeviceIdType.MESH
LANES = 128
SIDE = 2 * FOOT


def take(x, idx):
    return jnp.take_along_axis(x, idx, axis=1, mode="promise_in_bounds")


def iota(shape, dim):
    return lax.broadcasted_iota(jnp.int32, shape, dim)


def kernel(
    sizes,
    corner,
    owner,
    c_src,
    c_shift,
    c_start,
    f_src,
    f_shift,
    f_start,
    pot_out,
    fine_out,
    norm_out,
    U,
    W,
    comp,
    yh,
    ys,
    zh,
    zs,
    V,
    FW,
    FS,
    G,
    compact,
    R,
    pout,
    prec,
    rout,
    rrec,
    slotid,
    sums,
    xsum,
    p_send,
    p_recv,
    r_send,
    r_recv,
    h_send,
    h_recv,
    n_send,
    n_recv,
):
    n_gx, n_gy, n_gz = sizes
    group = n_gy * n_gz
    slots = owner.shape[1]
    nx, ny, nz = c_src.shape
    along_y = ny // FOOT
    gx, gy, gz = lax.axis_index("gx"), lax.axis_index("gy"), lax.axis_index("gz")
    me = gy * n_gz + gz

    def rank_id(rank):
        return (gx, rank // n_gz, rank % n_gz)

    have = (gx > 0, gx < n_gx - 1, gy > 0, gy < n_gy - 1, gz > 0, gz < n_gz - 1)
    beside = (
        (gx - 1, gy, gz),
        (gx + 1, gy, gz),
        (gx, gy - 1, gz),
        (gx, gy + 1, gz),
        (gx, gy, gz - 1),
        (gx, gy, gz + 1),
    )

    for p in range(2):
        U[p, 0] = jnp.zeros((ny, nz), jnp.float32)
        U[p, nx + 1] = jnp.zeros((ny, nz), jnp.float32)
    yh[...] = jnp.zeros_like(yh)
    zh[...] = jnp.zeros_like(zh)

    barrier = pltpu.get_barrier_semaphore()
    for d in range(1, group):
        pl.semaphore_signal(barrier, inc=1, device_id=rank_id((me + d) % group), device_id_type=MESH)
    for d in range(1, n_gx):
        pl.semaphore_signal(barrier, inc=1, device_id=((gx + d) % n_gx, gy, gz), device_id_type=MESH)
    pl.semaphore_wait(barrier, group - 1 + n_gx - 1)

    tile = (8, LANES)
    lane = iota(tile, 1)
    sub = iota(tile, 0)
    wide = (ny, LANES)
    wlane = iota(wide, 1)
    wsub = iota(wide, 0)
    box_row = []
    box_col = []
    box_live = []
    for s in range(slots):
        box_row.append((corner[0, s, 1] // 2 - gy * ny) // FOOT)
        box_col.append((corner[0, s, 2] // 2 - gz * nz) // FOOT)
        box_live.append(owner[0, s] < group)

    def exchange(out, rec, send, recv, rows):
        copies = []
        for d in range(1, group):
            peer = (me + d) % group
            copy = pltpu.make_async_remote_copy(
                src_ref=out.at[peer, pl.ds(0, rows)],
                dst_ref=rec.at[me, pl.ds(0, rows)],
                send_sem=send.at[d],
                recv_sem=recv.at[d],
                device_id=rank_id(peer),
                device_id_type=MESH,
            )
            copy.start()
            copies.append(copy)
        rec[me, pl.ds(0, rows)] = out[me, pl.ds(0, rows)]
        return copies

    def arrive(out, rec, send, recv, rows):
        for d in range(1, group):
            source = (me + group - d) % group
            pltpu.make_async_remote_copy(
                src_ref=out.at[source, pl.ds(0, rows)],
                dst_ref=rec.at[source, pl.ds(0, rows)],
                send_sem=send.at[d],
                recv_sem=recv.at[d],
                device_id=rank_id(source),
                device_id_type=MESH,
            ).wait_recv()

    def pack_parents(p):
        @pl.loop(0, FOOT // 4)
        def _(xg):
            for s in range(slots):
                idx = box_col[s] * FOOT + (lane % FOOT)
                acc = jnp.zeros(tile, jnp.float32)
                for k in range(4):
                    for yl in range(2):
                        a = U[p, 1 + xg * 4 + k, pl.ds(yl, 8, stride=2), :]
                        for b in range(1, along_y):
                            other = U[p, 1 + xg * 4 + k, pl.ds(b * FOOT + yl, 8, stride=2), :]
                            a = jnp.where(box_row[s] == b, other, a)
                        acc = jnp.where(lane // FOOT == 2 * k + yl, take(a, idx), acc)
                compact[s, pl.ds(pl.multiple_of(xg * 8, 8), 8), :] = acc

        for q in range(group):
            acc = jnp.zeros((32, LANES), jnp.float32)
            flag = jnp.zeros(tile, jnp.float32)
            for s in range(slots):
                acc = jnp.where(owner[0, s] == q, compact[s], acc)
                flag = jnp.where(owner[0, s] == q, 1.0, flag)
            pout[q, pl.ds(0, 32)] = acc
            pout[q, pl.ds(32, 8)] = flag

    def slot_masks():
        count = jnp.zeros(tile, jnp.float32)
        for q in range(group):
            flag = prec[q, pl.ds(32, 8)]
            slotid[q] = jnp.where(flag > 0.5, count, -1.0)
            count = count + flag
        return count

    spread_lane = (lane // 64) * FOOT + (lane % SIDE) // 2

    def ghosts(par):
        @pl.loop(0, FOOT // 4)
        def _(xg):
            rows = pl.ds(pl.multiple_of(xg * 8, 8), 8)
            for j in range(slots):
                acc = jnp.zeros(tile, jnp.float32)
                for q in range(group):
                    acc = jnp.where(slotid[q] == float(j), prec[q, rows], acc)
                for k in range(4):
                    G[par, j, xg * 4 + k] = take(acc, k * SIDE + spread_lane)

    y_top = (lane >= 96) & (sub == 7)
    y_low = (lane < 32) & (sub == 0)
    z_pos = lane % SIDE

    def beside_fine(vp, par, j, x, ghost):
        v = V[vp, j, x + 1]
        up = pltpu.roll(v, LANES - 32, 1)
        up = jnp.where(lane < 96, up, pltpu.roll(up, 7, 0))
        up = jnp.where(y_top, ghost, up)
        lo = pltpu.roll(v, 32, 1)
        lo = jnp.where(lane >= 32, lo, pltpu.roll(lo, 1, 0))
        lo = jnp.where(y_low, ghost, lo)
        zu = jnp.where(z_pos < SIDE - 1, pltpu.roll(v, LANES - 1, 1), ghost)
        zl = jnp.where(z_pos > 0, pltpu.roll(v, 1, 1), ghost)
        return v, ((V[vp, j, x + 2] + V[vp, j, x]) + (up + lo)) + (zu + zl)

    def fine_rows(j, x):
        return pl.ds(x * 8 * slots + j, 8, stride=slots)

    def edges(vp, par):
        for j in range(slots):
            V[vp, j, 0] = G[par, j, 0]
            V[vp, j, SIDE + 1] = G[par, j, FOOT - 1]

    def fine_sweep(vp, par):
        @pl.loop(0, FOOT)
        def _(X):
            for j in range(slots):
                ghost = G[par, j, X]
                for e in range(2):
                    x = 2 * X + e
                    v, s = beside_fine(vp, par, j, x, ghost)
                    V[1 - vp, j, x + 1] = KEEP * v + FW[j, x] * (FS[j, x] + s)

    shrink_lane = ((lane % 32) // FOOT) * 64 + 2 * (lane % FOOT)

    def fine_remainder(vp, par, occupied):
        def body(xg, total):
            for j in range(slots):
                acc = jnp.zeros(tile, jnp.float32)
                for k in range(4):
                    X = xg * 4 + k
                    ghost = G[par, j, X]
                    t = None
                    for e in range(2):
                        x = 2 * X + e
                        v, s = beside_fine(vp, par, j, x, ghost)
                        r = (FS[j, x] - (6.0 + f_shift[fine_rows(j, x), :]) * v) + s
                        r = jnp.where(occupied[j], r, 0.0)
                        total = total + r * r
                        t = r if t is None else t + r
                    t = t + pltpu.roll(t, LANES - 1, 1)
                    t = t + pltpu.roll(t, LANES - 32, 1)
                    acc = jnp.where(lane // 32 == k, take(t, shrink_lane), acc)
                R[j, pl.ds(pl.multiple_of(xg * 8, 8), 8), :] = acc * 0.125
            return total

        return lax.fori_loop(0, FOOT // 4, body, jnp.zeros(tile, jnp.float32))

    def pack_returns():
        for q in range(group):
            which = slotid[q]
            for g in range(4):
                rows = pl.ds(g * 8, 8)
                acc = jnp.zeros(tile, jnp.float32)
                for j in range(slots):
                    acc = jnp.where(which == float(j), R[j, rows], acc)
                rout[q, rows] = acc

    def deposit():
        @pl.loop(0, FOOT // 4)
        def _(xg):
            rows = pl.ds(pl.multiple_of(xg * 8, 8), 8)
            tiles = []
            for s in range(slots):
                tiles.append(rrec[jnp.minimum(owner[0, s], group - 1), rows])
            for k in range(4):
                x = xg * 4 + k
                for yl in range(2):
                    idx = k * 32 + yl * FOOT + lane % FOOT
                    got = []
                    for s in range(slots):
                        col = jnp.where(box_live[s], box_col[s], -1)
                        got.append(jnp.where(lane // FOOT == col, take(tiles[s], idx), 0.0))
                    for b in range(along_y):
                        place = pl.ds(b * FOOT + yl, 8, stride=2)
                        acc = c_src[x, place, :]
                        for s in range(slots):
                            acc = acc + jnp.where(box_row[s] == b, got[s], 0.0)
                        comp[x, place, :] = acc

    def halo_copies(p):
        faces = (
            (U.at[p, 1], U.at[p, nx + 1]),
            (U.at[p, nx], U.at[p, 0]),
            (ys.at[0], yh.at[p, 1]),
            (ys.at[1], yh.at[p, 0]),
            (zs.at[0], zh.at[p, 1]),
            (zs.at[1], zh.at[p, 0]),
        )
        copies = []
        for i, (source, target) in enumerate(faces):
            copies.append(
                pltpu.make_async_remote_copy(
                    src_ref=source,
                    dst_ref=target,
                    send_sem=h_send.at[p, i],
                    recv_sem=h_recv.at[p, i ^ 1],
                    device_id=beside[i],
                    device_id_type=MESH,
                )
            )
        return copies

    def halo_waits(p):
        places = (
            U.at[p, 0],
            U.at[p, nx + 1],
            yh.at[p, 0],
            yh.at[p, 1],
            zh.at[p, 0],
            zh.at[p, 1],
        )
        copies = []
        for i, target in enumerate(places):
            copies.append(
                pltpu.make_async_remote_copy(
                    src_ref=target,
                    dst_ref=target,
                    send_sem=h_send.at[p, i],
                    recv_sem=h_recv.at[p, i],
                    device_id=beside[i],
                    device_id_type=MESH,
                )
            )
        return copies

    def send_halos(p):
        for i, copy in enumerate(halo_copies(p)):
            pl.when(have[i])(copy.start)

    def wait_halos(p):
        for i, (sent, got) in enumerate(zip(halo_copies(p), halo_waits(p))):

            @pl.when(have[i])
            def _():
                sent.wait_send()
                got.wait_recv()

    def keep_faces(x, u, zlo, zhi):
        ys[0, pl.ds(x, 1), :] = u[0:1]
        ys[1, pl.ds(x, 1), :] = u[ny - 1 : ny]
        zlo = jnp.where(wlane == x, u[:, 0:1], zlo)
        zhi = jnp.where(wlane == x, u[:, nz - 1 : nz], zhi)
        return zlo, zhi

    none = jnp.zeros(wide, jnp.float32)

    def coarse_sweep(p, want_faces, want_square):
        zl = zh[p, 0]
        zu = zh[p, 1]

        zlo, zhi, total = none, none, none
        for x in range(nx):
            u = U[p, x + 1]
            ym = jnp.where(wsub == 0, yh[p, 0, pl.ds(x, 1), :], pltpu.roll(u, 1, 0))
            yp = jnp.where(wsub == ny - 1, yh[p, 1, pl.ds(x, 1), :], pltpu.roll(u, ny - 1, 0))
            zm = jnp.where(wlane == 0, pltpu.roll(zl, (LANES - x) % LANES, 1) if x else zl, pltpu.roll(u, 1, 1))
            zp = jnp.where(wlane == nz - 1, pltpu.roll(zu, LANES - 1 - x, 1), pltpu.roll(u, nz - 1, 1))
            s = ((U[p, x] + U[p, x + 2]) + (ym + yp)) + (zm + zp)
            s = s + comp[x]
            new = KEEP * u + W[x] * s
            U[1 - p, x + 1] = new
            if want_square:
                last = s - (6.0 + c_shift[x]) * u
                total = total + last * last
            if want_faces:
                zlo, zhi = keep_faces(x, new, zlo, zhi)
        if want_faces:
            zs[0] = zlo
            zs[1] = zhi
        return total

    zlo, zhi = none, none
    for x in range(nx):
        u = c_start[x]
        U[0, x + 1] = u
        zlo, zhi = keep_faces(x, u, zlo, zhi)
    zs[0] = zlo
    zs[1] = zhi
    pack_parents(0)
    parent_copies = exchange(pout, prec, p_send, p_recv, 40)
    send_halos(0)

    @pl.loop(0, nx)
    def _(x):
        W[x] = OMEGA / (6.0 + c_shift[x])

    @pl.loop(0, SIDE)
    def _(x):
        for j in range(slots):
            rows = fine_rows(j, x)
            V[0, j, x + 1] = f_start[rows, :]
            FS[j, x] = f_src[rows, :]
            FW[j, x] = OMEGA / (6.0 + f_shift[rows, :])

    vp = 0
    return_copies = []
    for cycle in range(CYCLES):
        par = cycle % 2
        arrive(pout, prec, p_send, p_recv, 40)
        if cycle == 0:
            count = slot_masks()
            occupied = [count > float(j) for j in range(slots)]
        ghosts(par)
        if cycle > 0:

            @pl.loop(0, FOOT)
            def _(X):
                for j in range(slots):
                    delta = G[par, j, X] - G[1 - par, j, X]
                    for e in range(2):
                        V[vp, j, 2 * X + e + 1] = V[vp, j, 2 * X + e + 1] + delta

        edges(0, par)
        edges(1, par)
        for sweep in range(FSWEEPS):
            fine_sweep(vp, par)
            vp = 1 - vp
        square = fine_remainder(vp, par, occupied)
        for copy in return_copies:
            copy.wait_send()
        pack_returns()
        return_copies = exchange(rout, rrec, r_send, r_recv, 32)
        arrive(rout, rrec, r_send, r_recv, 32)
        deposit()
        for sweep in range(CSWEEPS):
            p = sweep % 2
            final = cycle == CYCLES - 1 and sweep == CSWEEPS - 1
            wait_halos(p)
            total = coarse_sweep(p, not final, sweep == CSWEEPS - 1)
            if not final and sweep < CSWEEPS - 1:
                send_halos(1 - p)
        for g in range(ny // 8):
            square = square + total[8 * g : 8 * g + 8]
        sums[cycle] = square
        for copy in parent_copies:
            copy.wait_send()
        pack_parents(0)
        if cycle == CYCLES - 1:
            both = jnp.where(
                sub == 0,
                jnp.sum(sums[0], axis=0, keepdims=True),
                jnp.where(sub == 1, jnp.sum(sums[1], axis=0, keepdims=True), 0.0),
            )
            for q in range(group):
                pout[q, pl.ds(32, 8)] = both
        parent_copies = exchange(pout, prec, p_send, p_recv, 40)
        if cycle < CYCLES - 1:
            send_halos(0)

    @pl.loop(0, nx)
    def _(x):
        pot_out[x] = U[0, x + 1]

    for copy in return_copies:
        copy.wait_send()
    arrive(pout, prec, p_send, p_recv, 40)
    for copy in parent_copies:
        copy.wait_send()

    mine = jnp.zeros(tile, jnp.float32)
    for q in range(group):
        mine = mine + prec[q, pl.ds(32, 8)]
    xsum[gx] = mine
    norm_copies = []
    for d in range(1, n_gx):
        copy = pltpu.make_async_remote_copy(
            src_ref=xsum.at[gx],
            dst_ref=xsum.at[gx],
            send_sem=n_send.at[d],
            recv_sem=n_recv.at[d],
            device_id=((gx + d) % n_gx, gy, gz),
            device_id_type=MESH,
        )
        copy.start()
        norm_copies.append(copy)

    par = CYCLES % 2
    ghosts(par)

    @pl.loop(0, FOOT)
    def _(X):
        for j in range(slots):
            delta = G[par, j, X] - G[1 - par, j, X]
            for e in range(2):
                x = 2 * X + e
                fine_out[fine_rows(j, x), :] = jnp.where(occupied[j], V[vp, j, x + 1] + delta, 0.0)

    for d in range(1, n_gx):
        source = (gx + n_gx - d) % n_gx
        pltpu.make_async_remote_copy(
            src_ref=xsum.at[source],
            dst_ref=xsum.at[source],
            send_sem=n_send.at[d],
            recv_sem=n_recv.at[d],
            device_id=(source, gy, gz),
            device_id_type=MESH,
        ).wait_recv()
    for copy in norm_copies:
        copy.wait_send()
    whole = jnp.zeros(tile, jnp.float32)
    for d in range(n_gx):
        whole = whole + xsum[d]
    cells = float(nx * ny * nz * n_gx * group)
    whole = jnp.sum(whole, axis=1, keepdims=True) / cells
    norm_out[...] = jnp.broadcast_to(jnp.sqrt(whole), tile)


def to_rows(a):
    slots, fine = a.shape
    return a.reshape(slots, fine // LANES, LANES).transpose(1, 0, 2).reshape(slots * fine // LANES, LANES)


def from_rows(a, slots):
    return a.reshape(-1, slots, LANES).transpose(1, 0, 2).reshape(slots, -1)


def local(sizes, c_src, c_shift, c_start, f_src, f_shift, f_start, corner, owner):
    n_gx, n_gy, n_gz = sizes
    group = n_gy * n_gz
    slots = owner.shape[1]
    nx, ny, nz = c_src.shape
    fine = f_src.shape[1]
    f32 = jnp.float32
    vmem = pl.BlockSpec(memory_space=pltpu.VMEM)
    smem = pl.BlockSpec(memory_space=pltpu.SMEM)
    dma = pltpu.SemaphoreType.DMA
    pot, rows, norms = pl.pallas_call(
        functools.partial(kernel, sizes),
        out_shape=(
            jax.ShapeDtypeStruct((nx, ny, nz), f32),
            jax.ShapeDtypeStruct((slots * fine // LANES, LANES), f32),
            jax.ShapeDtypeStruct((8, LANES), f32),
        ),
        in_specs=[smem, smem] + [vmem] * 6,
        out_specs=(vmem, vmem, vmem),
        scratch_shapes=[
            pltpu.VMEM((2, nx + 2, ny, nz), f32),
            pltpu.VMEM((nx, ny, nz), f32),
            pltpu.VMEM((nx, ny, nz), f32),
            pltpu.VMEM((2, 2, nx, nz), f32),
            pltpu.VMEM((2, nx, nz), f32),
            pltpu.VMEM((2, 2, ny, nz), f32),
            pltpu.VMEM((2, ny, nz), f32),
            pltpu.VMEM((2, slots, SIDE + 2, 8, LANES), f32),
            pltpu.VMEM((slots, SIDE, 8, LANES), f32),
            pltpu.VMEM((slots, SIDE, 8, LANES), f32),
            pltpu.VMEM((2, slots, FOOT, 8, LANES), f32),
            pltpu.VMEM((slots, 32, LANES), f32),
            pltpu.VMEM((slots, 32, LANES), f32),
            pltpu.VMEM((group, 40, LANES), f32),
            pltpu.VMEM((group, 40, LANES), f32),
            pltpu.VMEM((group, 32, LANES), f32),
            pltpu.VMEM((group, 32, LANES), f32),
            pltpu.VMEM((group, 8, LANES), f32),
            pltpu.VMEM((CYCLES, 8, LANES), f32),
            pltpu.VMEM((n_gx, 8, LANES), f32),
            dma((group,)),
            dma((group,)),
            dma((group,)),
            dma((group,)),
            dma((2, 6)),
            dma((2, 6)),
            dma((n_gx,)),
            dma((n_gx,)),
        ],
        compiler_params=pltpu.CompilerParams(collective_id=0, has_side_effects=True),
    )(corner, owner, c_src, c_shift, c_start, to_rows(f_src), to_rows(f_shift), to_rows(f_start))
    return pot, from_rows(rows, slots), norms[:CYCLES, 0]


def solution(mesh):
    sizes = (mesh.shape["gx"], mesh.shape["gy"], mesh.shape["gz"])
    everywhere = ("gx", "gy", "gz")
    block = P(*everywhere)
    in_specs = (
        block,
        block,
        block,
        P(everywhere, None),
        P(everywhere, None),
        P(everywhere, None),
        P(everywhere, None, None),
        P(everywhere, None),
    )
    out_specs = (block, P(everywhere, None), P())
    return jax.shard_map(
        functools.partial(local, sizes), mesh=mesh, in_specs=in_specs, out_specs=out_specs, check_vma=False
    )
```

time: 507 us -> 81.2 us (0.16); the launches traced: 499 us -> 81 us
  local copies, waits for them, and re-layouts: 159 us -> 5.16 us
  starting transfers between devices: 138 us -> 0 us
  other arithmetic: 86.4 us -> 0 us
  Pallas kernels: 0 us -> 75.2 us
  waiting for transfers between devices: 54.9 us -> 0 us
  blocking collectives: 43.1 us -> 0 us
  matrix products: 13.1 us -> 0 us
    ppermute x42 -> x0, starting transfers between devices: 115 us -> none  [the longest x21 86.7 us: extended(): lax.ppermute(lax.slice_in_dim(block, block.shape[dim] - width, None, axis...]
    pallas_call x0 -> x1, Pallas kernels: none -> 75.2 us  [local(): pl.pallas_call(functools.partial(kernel, sizes), out_shape=(jax.ShapeDtyp...]
    reshape x15 -> x0, local copies, waits for them, and re-layouts: 62.8 us -> none  [the longest x4 38 us: inject(): return spread.reshape(number, 8 * FOOT * FOOT * FOOT)]
    ppermute x42 -> x0, waiting for transfers between devices: 54.9 us -> none  [the longest x21 27.5 us: extended(): lax.ppermute(lax.slice_in_dim(block, 0, width, axis=dim), axis, backward)]
    broadcast_in_dim x8 -> x0, local copies, waits for them, and re-layouts: 45.1 us -> none  [inject(): spread = jnp.broadcast_to(shaped, (number, FOOT, 2, FOOT, 2, FOOT, 2))]
    psum x1 -> x0, blocking collectives: 43.1 us -> none  [local(): norms.append(lax.psum(local_sum, ('gx', 'gy', 'gz')))]
    reduce_sum x7 -> x0, other arithmetic: 34.5 us -> none  [the longest x2 27.5 us: restrict(): return values.reshape(number, FOOT, 2, FOOT, 2, FOOT, 2).mean(axis=(2, 4,...]
    add x16 -> x0, other arithmetic: 23.3 us -> none  [the longest x6 18.1 us: local(): values + OMEGA * fine_residual(values, parents, fine_source, fine_shift)...]
  transfers between devices with their start and end apart: 48 -> 0, of which waited for: 16 -> 0; matrix products, arithmetic and copies ran while one was open for 41% -> 0% of each run, Pallas kernels for 0% -> 0%
where the time goes in v1:
time: 81.2 us; the launch traced here: 81 us
  Pallas kernels  75.2 us (93%)
  local copies, waits for them, and re-layouts  5.16 us (6%)
    pallas_call x1, Pallas kernels, local(): pl.pallas_call(functools.partial(kernel, sizes), out_shape=(jax.ShapeDtyp...  75.2 us
    unnamed x7, local copies, waits for them, and re-layouts  3.8 us

profile of v1, /device:TPU:0, one launch (start us, length us, event | category | flops | bytes accessed | tf_op | source)
XLA Modules:
  0.0 81.0 jit_solution(1605786169912482722)
XLA Ops:
  0.6 0.0 copy-start.1
  0.6 0.7 copy-done.1
  1.3 0.7 copy.19.corner
  2.0 75.2 %shard_map.103 = (f32[16,32,128]{2,1,0:T(8,128)}, f32[1024,128]{1,0:T(8,128)}, f32[8,128]{1,0:T(8,128)}) custom-call(s32[1,4,3]{2,1,0:T(4,128)} %copy.19.corner, s32[1,4]{1,0:T(1,128)} %owner.1, f32[16,32,128]{2,1,0:T(8,128)} %c_src.1, f32[16,32,128]{2,1,0:T(8,128)} %c_shift.1, f32[16,32,128]{2,1,0:T(8,128)} %c_start.1, f32[1024,128]{1,0:T(8,128)} %bitcast.21, ...), custom_call_target="tpu_custom_call" | custom-call | tf_op jit(solution)/shard_map/pallas_call | solution.py:531
  77.1 0.0 copy-start
  77.1 1.4 %slice_reduce_fusion = f32[2]{0:T(128)} fusion(f32[8,128]{1,0:T(8,128)} %get-tuple-element.8), kind=kLoop, calls=%fused_computation | loop fusion | bytes 16 | tf_op jit(solution)/shard_map/slice | solution.py:572
  78.5 1.7 %copy.23 = f32[16,32,128]{2,1,0:T(8,128)} copy(f32[16,32,128]{2,1,0:T(8,128)} %get-tuple-element.12) | data formatting | bytes 524288
  80.2 0.0 copy-done
  80.2 0.8 copy.24
Async XLA Ops:
  0.6 0.7 copy-start.1
  77.1 3.0 %copy-start = (f32[1024,128]{1,0:T(8,128)S(1)}, f32[1024,128]{1,0:T(8,128)}, u32[]{:S(2)}) copy-start(f32[1024,128]{1,0:T(8,128)} %get-tuple-element.7) | copy-start | bytes 1572868

commit v2 on v1

--- a/solution.py
+++ b/solution.py
@@ -30,15 +30,21 @@
     sizes,
     corner,
     owner,
+    c_src_hbm,
+    c_shift_hbm,
+    c_start_hbm,
+    f_src_hbm,
+    f_shift_hbm,
+    f_start_hbm,
+    pot_out,
+    fine_out,
+    norm_out,
     c_src,
     c_shift,
-    c_start,
     f_src,
     f_shift,
     f_start,
-    pot_out,
-    fine_out,
-    norm_out,
+    in_sem,
     U,
     W,
     comp,
@@ -49,6 +55,7 @@
     V,
     FW,
     FS,
+    FD,
     G,
     compact,
     R,
@@ -71,7 +78,7 @@
     n_gx, n_gy, n_gz = sizes
     group = n_gy * n_gz
     slots = owner.shape[1]
-    nx, ny, nz = c_src.shape
+    nx, ny, nz = c_src_hbm.shape
     along_y = ny // FOOT
     gx, gy, gz = lax.axis_index("gx"), lax.axis_index("gy"), lax.axis_index("gz")
     me = gy * n_gz + gz
@@ -88,6 +95,22 @@
         (gx, gy, gz - 1),
         (gx, gy, gz + 1),
     )
+
+    loads = [
+        pltpu.make_async_copy(source, target, in_sem.at[i])
+        for i, (source, target) in enumerate(
+            (
+                (c_start_hbm, U.at[0, pl.ds(1, nx)]),
+                (c_shift_hbm, c_shift),
+                (f_start_hbm, f_start),
+                (f_src_hbm, f_src),
+                (f_shift_hbm, f_shift),
+                (c_src_hbm, c_src),
+            )
+        )
+    ]
+    for load in loads:
+        load.start()
 
     for p in range(2):
         U[p, 0] = jnp.zeros((ny, nz), jnp.float32)
@@ -112,8 +135,8 @@
     box_col = []
     box_live = []
     for s in range(slots):
-        box_row.append((corner[0, s, 1] // 2 - gy * ny) // FOOT)
-        box_col.append((corner[0, s, 2] // 2 - gz * nz) // FOOT)
+        box_row.append((corner[1, 0, s] // 2 - gy * ny) // FOOT)
+        box_col.append((corner[2, 0, s] // 2 - gz * nz) // FOOT)
         box_live.append(owner[0, s] < group)
 
     def exchange(out, rec, send, recv, rows):
@@ -194,60 +217,72 @@
     y_low = (lane < 32) & (sub == 0)
     z_pos = lane % SIDE
 
+    def plane(x, shift=0):
+        start = pl.multiple_of((x + 1) * 8, 8)
+        return pl.ds(start + shift, 8)
+
     def beside_fine(vp, par, j, x, ghost):
-        v = V[vp, j, x + 1]
-        up = pltpu.roll(v, LANES - 32, 1)
-        up = jnp.where(lane < 96, up, pltpu.roll(up, 7, 0))
-        up = jnp.where(y_top, ghost, up)
-        lo = pltpu.roll(v, 32, 1)
-        lo = jnp.where(lane >= 32, lo, pltpu.roll(lo, 1, 0))
-        lo = jnp.where(y_low, ghost, lo)
+        v = V[vp, j, plane(x)]
+        up = jnp.where(lane < 32, V[vp, j, plane(x, 1)], v)
+        up = jnp.where(y_top, ghost, pltpu.roll(up, LANES - 32, 1))
+        lo = jnp.where(lane >= 96, V[vp, j, plane(x, -1)], v)
+        lo = jnp.where(y_low, ghost, pltpu.roll(lo, 32, 1))
         zu = jnp.where(z_pos < SIDE - 1, pltpu.roll(v, LANES - 1, 1), ghost)
         zl = jnp.where(z_pos > 0, pltpu.roll(v, 1, 1), ghost)
-        return v, ((V[vp, j, x + 2] + V[vp, j, x]) + (up + lo)) + (zu + zl)
+        return v, ((V[vp, j, plane(x + 1)] + V[vp, j, plane(x - 1)]) + (up + lo)) + (zu + zl)
 
     def fine_rows(j, x):
         return pl.ds(x * 8 * slots + j, 8, stride=slots)
 
     def edges(vp, par):
         for j in range(slots):
-            V[vp, j, 0] = G[par, j, 0]
-            V[vp, j, SIDE + 1] = G[par, j, FOOT - 1]
+            V[vp, j, plane(-1)] = G[par, j, 0]
+            V[vp, j, plane(SIDE)] = G[par, j, FOOT - 1]
 
     def fine_sweep(vp, par):
-        @pl.loop(0, FOOT)
+        @pl.loop(0, FOOT, unroll=4)
         def _(X):
             for j in range(slots):
                 ghost = G[par, j, X]
                 for e in range(2):
                     x = 2 * X + e
                     v, s = beside_fine(vp, par, j, x, ghost)
-                    V[1 - vp, j, x + 1] = KEEP * v + FW[j, x] * (FS[j, x] + s)
+                    V[1 - vp, j, plane(x)] = KEEP * v + FW[j, x] * (FS[j, x] + s)
 
     shrink_lane = ((lane % 32) // FOOT) * 64 + 2 * (lane % FOOT)
 
     def fine_remainder(vp, par, occupied):
-        def body(xg, total):
+        def body(X, totals):
+            totals = list(totals)
             for j in range(slots):
-                acc = jnp.zeros(tile, jnp.float32)
+                ghost = G[par, j, X]
+                for e in range(2):
+                    x = 2 * X + e
+                    v, s = beside_fine(vp, par, j, x, ghost)
+                    r = (FS[j, x] - FD[j, x] * v) + s
+                    totals[j] = totals[j] + r * r
+                    V[1 - vp, j, plane(x)] = r
+            return tuple(totals)
+
+        zero = jnp.zeros(tile, jnp.float32)
+        totals = lax.fori_loop(0, FOOT, body, (zero,) * slots, unroll=4)
+
+        @pl.loop(0, FOOT // 4)
+        def _(xg):
+            for j in range(slots):
+                acc = zero
                 for k in range(4):
-                    X = xg * 4 + k
-                    ghost = G[par, j, X]
-                    t = None
-                    for e in range(2):
-                        x = 2 * X + e
-                        v, s = beside_fine(vp, par, j, x, ghost)
-                        r = (FS[j, x] - (6.0 + f_shift[fine_rows(j, x), :]) * v) + s
-                        r = jnp.where(occupied[j], r, 0.0)
-                        total = total + r * r
-                        t = r if t is None else t + r
+                    x = 2 * (xg * 4 + k)
+                    t = V[1 - vp, j, plane(x)] + V[1 - vp, j, plane(x + 1)]
                     t = t + pltpu.roll(t, LANES - 1, 1)
                     t = t + pltpu.roll(t, LANES - 32, 1)
                     acc = jnp.where(lane // 32 == k, take(t, shrink_lane), acc)
-                R[j, pl.ds(pl.multiple_of(xg * 8, 8), 8), :] = acc * 0.125
-            return total
-
-        return lax.fori_loop(0, FOOT // 4, body, jnp.zeros(tile, jnp.float32))
+                R[j, pl.ds(pl.multiple_of(xg * 8, 8), 8)] = acc * 0.125
+
+        total = zero
+        for j in range(slots):
+            total = total + jnp.where(occupied[j], totals[j], 0.0)
+        return total
 
     def pack_returns():
         for q in range(group):
@@ -281,7 +316,7 @@
                             acc = acc + jnp.where(box_row[s] == b, got[s], 0.0)
                         comp[x, place, :] = acc
 
-    def halo_copies(p):
+    def halo_copies(p, which=range(6)):
         faces = (
             (U.at[p, 1], U.at[p, nx + 1]),
             (U.at[p, nx], U.at[p, 0]),
@@ -291,7 +326,8 @@
             (zs.at[1], zh.at[p, 0]),
         )
         copies = []
-        for i, (source, target) in enumerate(faces):
+        for i in which:
+            source, target = faces[i]
             copies.append(
                 pltpu.make_async_remote_copy(
                     src_ref=source,
@@ -327,8 +363,8 @@
             )
         return copies
 
-    def send_halos(p):
-        for i, copy in enumerate(halo_copies(p)):
+    def send_halos(p, which):
+        for i, copy in zip(which, halo_copies(p, which)):
             pl.when(have[i])(copy.start)
 
     def wait_halos(p):
@@ -339,50 +375,75 @@
                 sent.wait_send()
                 got.wait_recv()
 
-    def keep_faces(x, u, zlo, zhi):
-        ys[0, pl.ds(x, 1), :] = u[0:1]
-        ys[1, pl.ds(x, 1), :] = u[ny - 1 : ny]
-        zlo = jnp.where(wlane == x, u[:, 0:1], zlo)
-        zhi = jnp.where(wlane == x, u[:, nz - 1 : nz], zhi)
-        return zlo, zhi
+    groups = ny // 8
+    per = min(groups, LANES // nx)
+
+    def keep_y(p):
+        for x in range(nx):
+            ys[0, pl.ds(x, 1), :] = U[p, x + 1, pl.ds(0, 1), :]
+            ys[1, pl.ds(x, 1), :] = U[p, x + 1, pl.ds(ny - 1, 1), :]
+
+    def keep_z(p):
+        for t in range(groups // per):
+
+            def body(x, faces):
+                zlo, zhi = faces
+                for g in range(per):
+                    at = g * nx + x
+                    u = U[p, x + 1, pl.ds((t * per + g) * 8, 8)]
+                    zlo = jnp.where(lane == at, pltpu.roll(u, at, 1), zlo)
+                    zhi = jnp.where(lane == at, pltpu.roll(u, (at + 1) % LANES, 1), zhi)
+                return zlo, zhi
+
+            empty = jnp.zeros(tile, jnp.float32)
+            zlo, zhi = lax.fori_loop(0, nx // 4, lambda i, f: body(4 * i + 3, body(4 * i + 2, body(4 * i + 1, body(4 * i, f)))), (empty, empty))
+            zs[0, pl.ds(t * 8, 8)] = zlo
+            zs[1, pl.ds(t * 8, 8)] = zhi
+
+    def send_faces(p):
+        send_halos(p, (0, 1))
+        keep_y(p)
+        send_halos(p, (2, 3))
+        keep_z(p)
+        send_halos(p, (4, 5))
+
+    def z_column(packed, x, to):
+        tiles = []
+        for g in range(groups):
+            at = (g % per) * nx + x
+            face = packed[8 * (g // per) : 8 * (g // per) + 8]
+            shift = (to - at) % LANES
+            tiles.append(pltpu.roll(face, shift, 1) if shift else face)
+        return jnp.concatenate(tiles, axis=0)
 
     none = jnp.zeros(wide, jnp.float32)
 
-    def coarse_sweep(p, want_faces, want_square):
+    def coarse_sweep(p, want_square):
         zl = zh[p, 0]
         zu = zh[p, 1]
 
-        zlo, zhi, total = none, none, none
+        total = none
         for x in range(nx):
             u = U[p, x + 1]
             ym = jnp.where(wsub == 0, yh[p, 0, pl.ds(x, 1), :], pltpu.roll(u, 1, 0))
             yp = jnp.where(wsub == ny - 1, yh[p, 1, pl.ds(x, 1), :], pltpu.roll(u, ny - 1, 0))
-            zm = jnp.where(wlane == 0, pltpu.roll(zl, (LANES - x) % LANES, 1) if x else zl, pltpu.roll(u, 1, 1))
-            zp = jnp.where(wlane == nz - 1, pltpu.roll(zu, LANES - 1 - x, 1), pltpu.roll(u, nz - 1, 1))
+            zm = jnp.where(wlane == 0, z_column(zl, x, 0), pltpu.roll(u, 1, 1))
+            zp = jnp.where(wlane == nz - 1, z_column(zu, x, nz - 1), pltpu.roll(u, nz - 1, 1))
             s = ((U[p, x] + U[p, x + 2]) + (ym + yp)) + (zm + zp)
             s = s + comp[x]
-            new = KEEP * u + W[x] * s
-            U[1 - p, x + 1] = new
+            U[1 - p, x + 1] = KEEP * u + W[x] * s
             if want_square:
                 last = s - (6.0 + c_shift[x]) * u
                 total = total + last * last
-            if want_faces:
-                zlo, zhi = keep_faces(x, new, zlo, zhi)
-        if want_faces:
-            zs[0] = zlo
-            zs[1] = zhi
         return total
 
-    zlo, zhi = none, none
-    for x in range(nx):
-        u = c_start[x]
-        U[0, x + 1] = u
-        zlo, zhi = keep_faces(x, u, zlo, zhi)
-    zs[0] = zlo
-    zs[1] = zhi
+    loads[0].wait()
     pack_parents(0)
     parent_copies = exchange(pout, prec, p_send, p_recv, 40)
-    send_halos(0)
+    send_faces(0)
+
+    for load in loads[1:]:
+        load.wait()
 
     @pl.loop(0, nx)
     def _(x):
@@ -392,9 +453,10 @@
     def _(x):
         for j in range(slots):
             rows = fine_rows(j, x)
-            V[0, j, x + 1] = f_start[rows, :]
+            V[0, j, plane(x)] = f_start[rows, :]
             FS[j, x] = f_src[rows, :]
-            FW[j, x] = OMEGA / (6.0 + f_shift[rows, :])
+            FD[j, x] = 6.0 + f_shift[rows, :]
+            FW[j, x] = OMEGA / FD[j, x]
 
     vp = 0
     return_copies = []
@@ -412,7 +474,7 @@
                 for j in range(slots):
                     delta = G[par, j, X] - G[1 - par, j, X]
                     for e in range(2):
-                        V[vp, j, 2 * X + e + 1] = V[vp, j, 2 * X + e + 1] + delta
+                        V[vp, j, plane(2 * X + e)] = V[vp, j, plane(2 * X + e)] + delta
 
         edges(0, par)
         edges(1, par)
@@ -430,9 +492,9 @@
             p = sweep % 2
             final = cycle == CYCLES - 1 and sweep == CSWEEPS - 1
             wait_halos(p)
-            total = coarse_sweep(p, not final, sweep == CSWEEPS - 1)
+            total = coarse_sweep(p, sweep == CSWEEPS - 1)
             if not final and sweep < CSWEEPS - 1:
-                send_halos(1 - p)
+                send_faces(1 - p)
         for g in range(ny // 8):
             square = square + total[8 * g : 8 * g + 8]
         sums[cycle] = square
@@ -449,11 +511,10 @@
                 pout[q, pl.ds(32, 8)] = both
         parent_copies = exchange(pout, prec, p_send, p_recv, 40)
         if cycle < CYCLES - 1:
-            send_halos(0)
-
-    @pl.loop(0, nx)
-    def _(x):
-        pot_out[x] = U[0, x + 1]
+            send_faces(0)
+
+    store = pltpu.make_async_copy(U.at[0, pl.ds(1, nx)], pot_out, in_sem.at[0])
+    store.start()
 
     for copy in return_copies:
         copy.wait_send()
@@ -487,7 +548,7 @@
             delta = G[par, j, X] - G[1 - par, j, X]
             for e in range(2):
                 x = 2 * X + e
-                fine_out[fine_rows(j, x), :] = jnp.where(occupied[j], V[vp, j, x + 1] + delta, 0.0)
+                fine_out[fine_rows(j, x), :] = jnp.where(occupied[j], V[vp, j, plane(x)] + delta, 0.0)
 
     for d in range(1, n_gx):
         source = (gx + n_gx - d) % n_gx
@@ -501,6 +562,7 @@
         ).wait_recv()
     for copy in norm_copies:
         copy.wait_send()
+    store.wait()
     whole = jnp.zeros(tile, jnp.float32)
     for d in range(n_gx):
         whole = whole + xsum[d]
@@ -525,6 +587,7 @@
     nx, ny, nz = c_src.shape
     fine = f_src.shape[1]
     f32 = jnp.float32
+    face_rows = ny // min(ny // 8, LANES // nx)
     vmem = pl.BlockSpec(memory_space=pltpu.VMEM)
     smem = pl.BlockSpec(memory_space=pltpu.SMEM)
     dma = pltpu.SemaphoreType.DMA
@@ -535,17 +598,24 @@
             jax.ShapeDtypeStruct((slots * fine // LANES, LANES), f32),
             jax.ShapeDtypeStruct((8, LANES), f32),
         ),
-        in_specs=[smem, smem] + [vmem] * 6,
-        out_specs=(vmem, vmem, vmem),
+        in_specs=[smem, smem] + [pl.BlockSpec(memory_space=pl.ANY)] * 6,
+        out_specs=(pl.BlockSpec(memory_space=pl.ANY), vmem, vmem),
         scratch_shapes=[
+            pltpu.VMEM((nx, ny, nz), f32),
+            pltpu.VMEM((nx, ny, nz), f32),
+            pltpu.VMEM((slots * fine // LANES, LANES), f32),
+            pltpu.VMEM((slots * fine // LANES, LANES), f32),
+            pltpu.VMEM((slots * fine // LANES, LANES), f32),
+            dma((6,)),
             pltpu.VMEM((2, nx + 2, ny, nz), f32),
             pltpu.VMEM((nx, ny, nz), f32),
             pltpu.VMEM((nx, ny, nz), f32),
             pltpu.VMEM((2, 2, nx, nz), f32),
             pltpu.VMEM((2, nx, nz), f32),
-            pltpu.VMEM((2, 2, ny, nz), f32),
-            pltpu.VMEM((2, ny, nz), f32),
-            pltpu.VMEM((2, slots, SIDE + 2, 8, LANES), f32),
+            pltpu.VMEM((2, 2, face_rows, nz), f32),
+            pltpu.VMEM((2, face_rows, nz), f32),
+            pltpu.VMEM((2, slots, (SIDE + 2) * 8, LANES), f32),
+            pltpu.VMEM((slots, SIDE, 8, LANES), f32),
             pltpu.VMEM((slots, SIDE, 8, LANES), f32),
             pltpu.VMEM((slots, SIDE, 8, LANES), f32),
             pltpu.VMEM((2, slots, FOOT, 8, LANES), f32),
@@ -568,7 +638,7 @@
             dma((n_gx,)),
         ],
         compiler_params=pltpu.CompilerParams(collective_id=0, has_side_effects=True),
-    )(corner, owner, c_src, c_shift, c_start, to_rows(f_src), to_rows(f_shift), to_rows(f_start))
+    )(corner.transpose(2, 0, 1), owner, c_src, c_shift, c_start, to_rows(f_src), to_rows(f_shift), to_rows(f_start))
     return pot, from_rows(rows, slots), norms[:CYCLES, 0]
 
 

time: 81.2 us -> 67.8 us (0.83)
  Pallas kernels: 75.2 us -> 63.2 us
  local copies, waits for them, and re-layouts: 5.16 us -> 3.83 us
    pallas_call x1, Pallas kernels: 75.2 us -> 63.2 us  [local(): pl.pallas_call(functools.partial(kernel, sizes), out_shape=(jax.ShapeDtyp...]
    unnamed x7 -> x4, local copies, waits for them, and re-layouts: 3.8 us -> 2.47 us
where the time goes in v2:
time: 67.8 us; the launch traced here: 67.6 us
  Pallas kernels  63.2 us (93%)
  local copies, waits for them, and re-layouts  3.83 us (6%)
    pallas_call x1, Pallas kernels, local(): pl.pallas_call(functools.partial(kernel, sizes), out_shape=(jax.ShapeDtyp...  63.2 us
    unnamed x4, local copies, waits for them, and re-layouts  2.47 us
    slice x1, local copies, waits for them, and re-layouts, local(): return (pot, from_rows(rows, slots), norms[:CYCLES, 0])  1.36 us

profile of v2, /device:TPU:0, one launch (start us, length us, event | category | flops | bytes accessed | tf_op | source)
XLA Modules:
  0.0 67.6 jit_solution(10054178494360923018)
XLA Ops:
  0.6 63.2 %shard_map.103 = (f32[16,32,128]{2,1,0:T(8,128)}, f32[1024,128]{1,0:T(8,128)}, f32[8,128]{1,0:T(8,128)}) custom-call(s32[3,1,4]{2,1,0:T(1,128)} %bitcast.25, s32[1,4]{1,0:T(1,128)} %owner.1, f32[16,32,128]{2,1,0:T(8,128)} %c_src_hbm.1, f32[16,32,128]{2,1,0:T(8,128)} %c_shift_hbm.1, f32[16,32,128]{2,1,0:T(8,128)} %c_start_hbm.1, f32[1024,128]{1,0:T(8,128)} %bitcast.22, ...), custom_call_target="tpu_custom_call" | custom-call | tf_op jit(solution)/shard_map/pallas_call | solution.py:594
  63.8 0.0 copy-start
  63.8 1.4 %slice_reduce_fusion = f32[2]{0:T(128)} fusion(f32[8,128]{1,0:T(8,128)} %get-tuple-element.8), kind=kLoop, calls=%fused_computation | loop fusion | bytes 16 | tf_op jit(solution)/shard_map/slice | solution.py:642
  65.2 1.7 %copy.21 = f32[16,32,128]{2,1,0:T(8,128)} copy(f32[16,32,128]{2,1,0:T(8,128)} %get-tuple-element.12) | data formatting | bytes 524288
  66.8 0.0 copy-done
  66.8 0.8 %copy.22 = f32[4,32768]{1,0:T(4,128)} copy(f32[4,32768]{1,0:T(4,128)S(1)} %bitcast.21) | data formatting | bytes 1048576
Async XLA Ops:
  63.8 3.0 %copy-start = (f32[1024,128]{1,0:T(8,128)S(1)}, f32[1024,128]{1,0:T(8,128)}, u32[]{:S(2)}) copy-start(f32[1024,128]{1,0:T(8,128)} %get-tuple-element.7) | copy-start | bytes 1572868

commit v3 on v2

--- a/solution.py
+++ b/solution.py
@@ -569,6 +569,30 @@
     cells = float(nx * ny * nz * n_gx * group)
     whole = jnp.sum(whole, axis=1, keepdims=True) / cells
     norm_out[...] = jnp.broadcast_to(jnp.sqrt(whole), tile)
+
+
+def finish(pieces, norms, pot, rows, pot_out, rows_out, norm_out, pot_buf, rows_buf, in_sem, out_sem):
+    parts = []
+    for k, (source, buf, target) in enumerate(((rows, rows_buf, rows_out), (pot, pot_buf, pot_out))):
+        count = source.shape[0] // pieces
+        for i in range(pieces):
+            at = pl.ds(i * count, count)
+            n = k * pieces + i
+            parts.append(
+                (
+                    pltpu.make_async_copy(source.at[at], buf.at[at], in_sem.at[n]),
+                    pltpu.make_async_copy(buf.at[at], target.at[at], out_sem.at[n]),
+                )
+            )
+    for load, _ in parts:
+        load.start()
+    for k in range(CYCLES):
+        norm_out[k] = norms[k, 0]
+    for load, store in parts:
+        load.wait()
+        store.start()
+    for _, store in parts:
+        store.wait()
 
 
 def to_rows(a):
@@ -639,7 +663,25 @@
         ],
         compiler_params=pltpu.CompilerParams(collective_id=0, has_side_effects=True),
     )(corner.transpose(2, 0, 1), owner, c_src, c_shift, c_start, to_rows(f_src), to_rows(f_shift), to_rows(f_start))
-    return pot, from_rows(rows, slots), norms[:CYCLES, 0]
+    pieces = 2
+    anywhere = pl.BlockSpec(memory_space=pl.ANY)
+    pot, rows, norms = pl.pallas_call(
+        functools.partial(finish, pieces),
+        out_shape=(
+            jax.ShapeDtypeStruct(pot.shape, f32),
+            jax.ShapeDtypeStruct(rows.shape, f32),
+            jax.ShapeDtypeStruct((CYCLES,), f32),
+        ),
+        in_specs=[smem, anywhere, anywhere],
+        out_specs=(anywhere, anywhere, smem),
+        scratch_shapes=[
+            pltpu.VMEM(pot.shape, f32),
+            pltpu.VMEM(rows.shape, f32),
+            dma((2 * pieces,)),
+            dma((2 * pieces,)),
+        ],
+    )(norms, pot, rows)
+    return pot, from_rows(rows, slots), norms
 
 
 def solution(mesh):

time: 67.8 us -> 67.1 us (0.990)
  local copies, waits for them, and re-layouts: 3.83 us -> 0 us
  Pallas kernels: 63.2 us -> 66.3 us
    pallas_call x0 -> x1, Pallas kernels: none -> 3.13 us  [local(): pl.pallas_call(functools.partial(finish, pieces), out_shape=(jax.ShapeDty...]
    unnamed x4 -> x0, local copies, waits for them, and re-layouts: 2.47 us -> none
    slice x1 -> x0, local copies, waits for them, and re-layouts: 1.36 us -> none  [local(): return (pot, from_rows(rows, slots), norms[:CYCLES, 0])]
where the time goes in v3:
time: 67.1 us; the launch traced here: 66.9 us
  Pallas kernels  66.3 us (99%)
    pallas_call x1, Pallas kernels, local(): pl.pallas_call(functools.partial(kernel, sizes), out_shape=(jax.ShapeDtyp...  63.1 us
    pallas_call x1, Pallas kernels, local(): pl.pallas_call(functools.partial(finish, pieces), out_shape=(jax.ShapeDty...  3.13 us

profile of v3, /device:TPU:0, one launch (start us, length us, event | category | flops | bytes accessed | tf_op | source)
XLA Modules:
  0.0 66.9 jit_solution(6241702339213888570)
XLA Ops:
  0.6 63.1 %shard_map.103 = (f32[16,32,128]{2,1,0:T(8,128)}, f32[1024,128]{1,0:T(8,128)}, f32[8,128]{1,0:T(8,128)}) custom-call(s32[3,1,4]{2,1,0:T(1,128)} %bitcast.24, s32[1,4]{1,0:T(1,128)} %owner.1, f32[16,32,128]{2,1,0:T(8,128)} %c_src_hbm.1, f32[16,32,128]{2,1,0:T(8,128)} %c_shift_hbm.1, f32[16,32,128]{2,1,0:T(8,128)} %c_start_hbm.1, f32[1024,128]{1,0:T(8,128)} %bitcast.21, ...), custom_call_target="tpu_custom_call" | custom-call | tf_op jit(solution)/shard_map/pallas_call | solution.py:618
  63.8 3.1 %shard_map.104 = (f32[16,32,128]{2,1,0:T(8,128)}, f32[1024,128]{1,0:T(8,128)}, f32[2]{0:T(128)}) custom-call(f32[8,128]{1,0:T(8,128)} %get-tuple-element.9.norms, f32[16,32,128]{2,1,0:T(8,128)} %get-tuple-element.10.pot, f32[1024,128]{1,0:T(8,128)} %get-tuple-element.11.rows), custom_call_target="tpu_custom_call" | custom-call | tf_op jit(solution)/shard_map/pallas_call | solution.py:668
